TPU v7x, 32 devices: a whole 2x2x4 slice. The times are simulated.
32 devices in a mesh: gx: 4 (over y, core), gy: 8 (over z, x).
Axes of the slice: x: 2, y: 2, z: 4, core: 2. Of those that a mesh axis runs over, the one named last changes fastest.
Arguments:
- source: float32 [64, 16, 1024], P(None, 'gx', 'gy'), may hold values from -6 to 6
- initial: float32 [64, 16, 1024], P(None, 'gx', 'gy'), may hold values from -6 to 6
- reaction: float32 [64, 16, 1024], P(None, 'gx', 'gy'), may hold values from 1 to 3
- stiffness: float32 [16, 1024], P('gx', 'gy'), may hold values from 0.5 to 2
- line_op: float32 [8, 8], replicated, may hold values from -1.6 to 5.6
- face_deriv: float32 [8], replicated, may hold values from -2 to 2
- wall_flags: int32 [4, 16, 1024], P(None, 'gx', 'gy'), may hold values 0 or 1
Outputs:
- hessenberg: float32 [6, 5], replicated
- krylov_basis: float32 [6, 64, 16, 1024], P(None, None, 'gx', 'gy')
All inputs are finite; a program needn't handle non-finite values. No bound on the sum of `wall_flags` on one device may be relied on, other than what follows from the above.
Results may differ from a plain program's by a relative error of at most 0.0003.
Values sent between devices are 32-bit elements; how exact they have to be, the bound alone decides.
A program may use at most 64 MiB of HBM per device.

v0:
```python
import jax
import jax.numpy as jnp
from jax import lax
from jax.sharding import PartitionSpec as P

P_SIZE = 8
ITERS = 5
TAU = 2.0
FLOOR = 0.1


def extended(array, sides, width):
    for axis, dim in sides:
        devices, length = (lax.axis_size(axis), array.shape[dim])
        up = [(i, (i + 1) % devices) for i in range(devices)]
        down = [(j, i) for i, j in up]
        last = lax.slice_in_dim(array, length - width, length, axis=dim)
        leading = lax.slice_in_dim(array, 0, width, axis=dim)
        before = lax.ppermute(last, axis, up)
        after = lax.ppermute(leading, axis, down)
        array = jnp.concatenate([before, array, after], axis=dim)
    return array


def local_total(values):
    return jnp.sum(jnp.sum(values, axis=0))


def x_traces(nodes, face_deriv):
    highest = lax.Precision.HIGHEST
    lower = jnp.einsum("c,cbxy->bxy", face_deriv, nodes, precision=highest)
    upper = jnp.einsum("c,cbxy->bxy", face_deriv[::-1], nodes, precision=highest)
    return jnp.stack([nodes[0], lower, nodes[-1], upper])


def y_traces(nodes, face_deriv):
    highest = lax.Precision.HIGHEST
    lower = jnp.einsum("c,acxy->axy", face_deriv, nodes, precision=highest)
    upper = jnp.einsum("c,acxy->axy", face_deriv[::-1], nodes, precision=highest)
    return jnp.stack([nodes[:, 0], lower, nodes[:, -1], upper])


def apply_op(field, reaction, stiffness, line_op, face_deriv, opened):
    highest = lax.Precision.HIGHEST
    nodes = field.reshape(P_SIZE, P_SIZE, field.shape[1], field.shape[2])
    interior = stiffness * (
        jnp.einsum("ac,cbxy->abxy", line_op, nodes, precision=highest)
        + jnp.einsum("bc,acxy->abxy", line_op, nodes, precision=highest)
    )
    padded = extended(nodes, (("gx", 2), ("gy", 3)), 1)
    xside = x_traces(padded, face_deriv)[:, :, :, 1:-1]
    yside = y_traces(padded, face_deriv)[:, :, 1:-1, :]
    x_own = xside[:, :, 1:-1]
    y_own = yside[:, :, :, 1:-1]
    east_nb = xside[0:2, :, 2:]
    west_nb = xside[2:4, :, :-2]
    north_nb = yside[0:2, :, :, 2:]
    south_nb = yside[2:4, :, :, :-2]
    add_east = TAU * (x_own[2] - opened[1] * east_nb[0]) + 0.5 * (x_own[3] - opened[1] * east_nb[1])
    add_west = TAU * (x_own[0] - opened[0] * west_nb[0]) + 0.5 * (x_own[1] - opened[0] * west_nb[1])
    add_north = TAU * (y_own[2] - opened[3] * north_nb[0]) + 0.5 * (
        y_own[3] - opened[3] * north_nb[1]
    )
    add_south = TAU * (y_own[0] - opened[2] * south_nb[0]) + 0.5 * (
        y_own[1] - opened[2] * south_nb[1]
    )
    result = reaction.reshape(nodes.shape) * nodes + interior
    result = result.at[0].add(add_west).at[P_SIZE - 1].add(add_east)
    result = result.at[:, 0].add(add_south).at[:, P_SIZE - 1].add(add_north)
    return result.reshape(field.shape)


def norm_scale(vector, total):
    squares = lax.psum(local_total(vector * vector), ("gx", "gy"))
    return jnp.sqrt(squares / total + FLOOR)


def body(source, initial, reaction, stiffness, line_op, face_deriv, wall_flags):
    highest = lax.Precision.HIGHEST
    total = float(
        P_SIZE
        * P_SIZE
        * source.shape[1]
        * lax.axis_size("gx")
        * source.shape[2]
        * lax.axis_size("gy")
    )
    opened = 1.0 - wall_flags.astype(jnp.float32)

    def operate(field):
        return apply_op(field, reaction, stiffness, line_op, face_deriv, opened)

    def products(basis, image):
        per_cell = jnp.einsum("kqxy,qxy->kxy", basis, image, precision=highest)
        return jnp.sum(per_cell, axis=(1, 2))

    first = source - operate(initial)
    basis = jnp.zeros((ITERS + 1,) + source.shape, jnp.float32)
    hessen = jnp.zeros((ITERS + 1, ITERS), jnp.float32)
    rows = lax.broadcasted_iota(jnp.int32, (ITERS + 1, ITERS), 0)
    cols = lax.broadcasted_iota(jnp.int32, (ITERS + 1, ITERS), 1)
    slots = lax.broadcasted_iota(jnp.int32, (ITERS + 1,), 0)

    def advance(step, carry):
        basis, hessen, pending = carry
        image = operate(pending)
        local = products(basis, image)
        projected, crossed, squares = lax.psum(
            (local, local_total(pending * image), local_total(pending * pending)), ("gx", "gy")
        )
        beta = jnp.sqrt(squares / total + FLOOR)
        basis = lax.dynamic_update_index_in_dim(basis, pending / beta, step, 0)
        coeffs = projected / (total * beta) + jnp.where(
            slots == step, crossed / (total * beta * beta), 0.0
        )
        pending = image / beta - jnp.einsum("k,kqxy->qxy", coeffs, basis, precision=highest)
        hessen = hessen + jnp.where(cols == step, coeffs[:, None], 0.0)
        hessen = hessen + jnp.where((rows == step) & (cols == step - 1), beta, 0.0)
        return (basis, hessen, pending)

    basis, hessen, pending = lax.fori_loop(0, ITERS, advance, (basis, hessen, first))
    beta = norm_scale(pending, total)
    basis = basis.at[ITERS].set(pending / beta)
    hessen = hessen + jnp.where((rows == ITERS) & (cols == ITERS - 1), beta, 0.0)
    return (hessen, basis)


def solution(mesh):
    return jax.shard_map(
        body,
        mesh=mesh,
        in_specs=(
            P(None, "gx", "gy"),
            P(None, "gx", "gy"),
            P(None, "gx", "gy"),
            P("gx", "gy"),
            P(),
            P(),
            P(None, "gx", "gy"),
        ),
        out_specs=(P(), P(None, None, "gx", "gy")),
        check_vma=False,
    )
```

profile of v0, /device:TPU:0, one launch (start us, length us, event | category | flops | bytes accessed | tf_op | source)
XLA Modules:
  0.0 408.1 jit_solution(16767970016116543631)
XLA Ops:
  8.2 3.1 collective-permute-start.7
  12.3 4.8 %collective-permute-done.6 = f32[8,8,6,1]{3,0,2,1:T(8,128)S(1)} collective-permute-done((f32[8,8,6,1]{3,0,2,1:T(8,128)S(1)}, f32[8,8,6,1]{3,0,2,1:T(8,128)S(1)}, u32[]{:S(2)}, u32[]{:S(2)}) %collective-permute-start.6) | collective-permute-done | bytes 1568 | tf_op jit(solution)/shard_map/ppermute | solution.py:19
  26.0 339.5 %while.31 = (s32[]{:T(128)}, f32[6,64,4,128]{3,2,1,0:T(4,128)S(1)}, f32[6,5]{1,0:T(8,128)S(1)}, f32[64,4,128]{2,1,0:T(4,128)S(1)}, f32[64,4,128]{2,0,1:T(8,128)S...) while((s32[]{:T(128)}, f32[6,64,4,128]{3,2,1,0:T(4,128)S(1)}, ...), condition=%wide.region_6.7_spmd.clone.clone, body=%wide.region_0.6_spmd.clone.clone.sunk | while | flops 14006069 | bytes 9489035 | solution.py:121
  29.6 2.8 collective-permute-start.2
  32.7 4.3 %collective-permute-done.2 = f32[8,8,6,1]{3,0,2,1:T(8,128)S(1)} collective-permute-done((f32[8,8,6,1]{3,0,2,1:T(8,128)S(1)}, f32[8,8,6,1]{3,0,2,1:T(8,128)S(1)}, u32[]{:S(2)}, u32[]{:S(2)}) %collective-permute-start.2) | collective-permute-done | bytes 1568 | tf_op jit(solution)/shard_map/while/body/eval_jaxpr/ppermute | solution.py:20
  37.0 5.2 %collective-permute-done.3 = f32[8,8,6,1]{3,0,2,1:T(8,128)S(1)} collective-permute-done((f32[8,8,6,1]{3,0,2,1:T(8,128)S(1)}, f32[8,8,6,1]{3,0,2,1:T(8,128)S(1)}, u32[]{:S(2)}, u32[]{:S(2)}) %collective-permute-start.3) | collective-permute-done | bytes 1568 | tf_op jit(solution)/shard_map/while/body/eval_jaxpr/ppermute | solution.py:19
  49.8 39.4 %all-reduce.2 = (f32[]{:T(128)}, f32[6]{0:T(128)S(1)}, f32[]{:T(128)}) all-reduce(f32[]{:T(128)} %get-tuple-element.835, f32[6]{0:T(128)S(1)} %convolution_bitcast_fusion.2, f32[]{:T(128)} %fusion.189), channel_id=1, replica_groups=mesh['gx'=4,'gy'=8] {'gx','gy'}, use_global_device_ids=true, to_apply=%region_2.2 | all-reduce | flops 8 | bytes 64 | tf_op jit(solution)/shard_map/while/body/eval_jaxpr/psum | solution.py:108
  96.8 3.9 collective-permute-start.2
  101.0 4.9 %collective-permute-done.2 = f32[8,8,6,1]{3,0,2,1:T(8,128)S(1)} collective-permute-done((f32[8,8,6,1]{3,0,2,1:T(8,128)S(1)}, f32[8,8,6,1]{3,0,2,1:T(8,128)S(1)}, u32[]{:S(2)}, u32[]{:S(2)}) %collective-permute-start.2) | collective-permute-done | bytes 1568 | tf_op jit(solution)/shard_map/while/body/eval_jaxpr/ppermute | solution.py:20
  105.9 5.1 %collective-permute-done.3 = f32[8,8,6,1]{3,0,2,1:T(8,128)S(1)} collective-permute-done((f32[8,8,6,1]{3,0,2,1:T(8,128)S(1)}, f32[8,8,6,1]{3,0,2,1:T(8,128)S(1)}, u32[]{:S(2)}, u32[]{:S(2)}) %collective-permute-start.3) | collective-permute-done | bytes 1568 | tf_op jit(solution)/shard_map/while/body/eval_jaxpr/ppermute | solution.py:19
  118.6 39.2 %all-reduce.2 = (f32[]{:T(128)}, f32[6]{0:T(128)S(1)}, f32[]{:T(128)}) all-reduce(f32[]{:T(128)} %get-tuple-element.835, f32[6]{0:T(128)S(1)} %convolution_bitcast_fusion.2, f32[]{:T(128)} %fusion.189), channel_id=1, replica_groups=mesh['gx'=4,'gy'=8] {'gx','gy'}, use_global_device_ids=true, to_apply=%region_2.2 | all-reduce | flops 8 | bytes 64 | tf_op jit(solution)/shard_map/while/body/eval_jaxpr/psum | solution.py:108
  165.4 3.9 collective-permute-start.2
  169.6 4.6 %collective-permute-done.2 = f32[8,8,6,1]{3,0,2,1:T(8,128)S(1)} collective-permute-done((f32[8,8,6,1]{3,0,2,1:T(8,128)S(1)}, f32[8,8,6,1]{3,0,2,1:T(8,128)S(1)}, u32[]{:S(2)}, u32[]{:S(2)}) %collective-permute-start.2) | collective-permute-done | bytes 1568 | tf_op jit(solution)/shard_map/while/body/eval_jaxpr/ppermute | solution.py:20
  174.2 4.9 %collective-permute-done.3 = f32[8,8,6,1]{3,0,2,1:T(8,128)S(1)} collective-permute-done((f32[8,8,6,1]{3,0,2,1:T(8,128)S(1)}, f32[8,8,6,1]{3,0,2,1:T(8,128)S(1)}, u32[]{:S(2)}, u32[]{:S(2)}) %collective-permute-start.3) | collective-permute-done | bytes 1568 | tf_op jit(solution)/shard_map/while/body/eval_jaxpr/ppermute | solution.py:19
  186.7 39.1 %all-reduce.2 = (f32[]{:T(128)}, f32[6]{0:T(128)S(1)}, f32[]{:T(128)}) all-reduce(f32[]{:T(128)} %get-tuple-element.835, f32[6]{0:T(128)S(1)} %convolution_bitcast_fusion.2, f32[]{:T(128)} %fusion.189), channel_id=1, replica_groups=mesh['gx'=4,'gy'=8] {'gx','gy'}, use_global_device_ids=true, to_apply=%region_2.2 | all-reduce | flops 8 | bytes 64 | tf_op jit(solution)/shard_map/while/body/eval_jaxpr/psum | solution.py:108
  233.3 3.9 collective-permute-start.2
  237.6 4.6 %collective-permute-done.2 = f32[8,8,6,1]{3,0,2,1:T(8,128)S(1)} collective-permute-done((f32[8,8,6,1]{3,0,2,1:T(8,128)S(1)}, f32[8,8,6,1]{3,0,2,1:T(8,128)S(1)}, u32[]{:S(2)}, u32[]{:S(2)}) %collective-permute-start.2) | collective-permute-done | bytes 1568 | tf_op jit(solution)/shard_map/while/body/eval_jaxpr/ppermute | solution.py:20
  242.1 4.9 %collective-permute-done.3 = f32[8,8,6,1]{3,0,2,1:T(8,128)S(1)} collective-permute-done((f32[8,8,6,1]{3,0,2,1:T(8,128)S(1)}, f32[8,8,6,1]{3,0,2,1:T(8,128)S(1)}, u32[]{:S(2)}, u32[]{:S(2)}) %collective-permute-start.3) | collective-permute-done | bytes 1568 | tf_op jit(solution)/shard_map/while/body/eval_jaxpr/ppermute | solution.py:19
  254.7 39.1 %all-reduce.2 = (f32[]{:T(128)}, f32[6]{0:T(128)S(1)}, f32[]{:T(128)}) all-reduce(f32[]{:T(128)} %get-tuple-element.835, f32[6]{0:T(128)S(1)} %convolution_bitcast_fusion.2, f32[]{:T(128)} %fusion.189), channel_id=1, replica_groups=mesh['gx'=4,'gy'=8] {'gx','gy'}, use_global_device_ids=true, to_apply=%region_2.2 | all-reduce | flops 8 | bytes 64 | tf_op jit(solution)/shard_map/while/body/eval_jaxpr/psum | solution.py:108
  301.3 3.9 collective-permute-start.2
  305.5 4.6 %collective-permute-done.2 = f32[8,8,6,1]{3,0,2,1:T(8,128)S(1)} collective-permute-done((f32[8,8,6,1]{3,0,2,1:T(8,128)S(1)}, f32[8,8,6,1]{3,0,2,1:T(8,128)S(1)}, u32[]{:S(2)}, u32[]{:S(2)}) %collective-permute-start.2) | collective-permute-done | bytes 1568 | tf_op jit(solution)/shard_map/while/body/eval_jaxpr/ppermute | solution.py:20
  310.1 4.9 %collective-permute-done.3 = f32[8,8,6,1]{3,0,2,1:T(8,128)S(1)} collective-permute-done((f32[8,8,6,1]{3,0,2,1:T(8,128)S(1)}, f32[8,8,6,1]{3,0,2,1:T(8,128)S(1)}, u32[]{:S(2)}, u32[]{:S(2)}) %collective-permute-start.3) | collective-permute-done | bytes 1568 | tf_op jit(solution)/shard_map/while/body/eval_jaxpr/ppermute | solution.py:19
  322.6 39.1 %all-reduce.2 = (f32[]{:T(128)}, f32[6]{0:T(128)S(1)}, f32[]{:T(128)}) all-reduce(f32[]{:T(128)} %get-tuple-element.835, f32[6]{0:T(128)S(1)} %convolution_bitcast_fusion.2, f32[]{:T(128)} %fusion.189), channel_id=1, replica_groups=mesh['gx'=4,'gy'=8] {'gx','gy'}, use_global_device_ids=true, to_apply=%region_2.2 | all-reduce | flops 8 | bytes 64 | tf_op jit(solution)/shard_map/while/body/eval_jaxpr/psum | solution.py:108
  366.2 40.3 %psum.52 = f32[]{:T(128)} all-reduce(f32[]{:T(128)} %multiply_reduce_fusion.2), channel_id=1, replica_groups=mesh['gx'=4,'gy'=8] {'gx','gy'}, use_global_device_ids=true, to_apply=%region_8.9 | all-reduce | flops 1 | bytes 8 | tf_op jit(solution)/shard_map/psum | solution.py:74
  (330 shorter events, 88.2 us)
Async XLA Ops:
  1.6 4.1 %collective-permute-start.4 = (f32[8,8,1,128]{3,0,2,1:T(8,128)S(1)}, f32[8,8,1,128]{3,0,2,1:T(8,128)S(1)}, u32[]{:S(2)}, u32[]{:S(2)}) collective-permute-start(f32[8,8,1,128]{3,0,2,1:T(8,128)S(1)} %copy.247), channel_id=1, source_target_pairs={{0,8},{8,16},{16,24},{24,0},{1,9},{9,17},{17,25},{25,1},{2,10},{10... | collective-permute-start | bytes 98312 | tf_op jit(solution)/shard_map/ppermute | solution.py:19
  2.2 3.7 collective-permute-start.5
  6.0 11.1 %collective-permute-start.6 = (f32[8,8,6,1]{3,0,2,1:T(8,128)S(1)}, f32[8,8,6,1]{3,0,2,1:T(8,128)S(1)}, u32[]{:S(2)}, u32[]{:S(2)}) collective-permute-start(f32[8,8,6,1]{3,0,2,1:T(8,128)S(1)} %get-tuple-element.682), channel_id=1, source_target_pairs={{0,1},{1,2},{2,3},{3,4},{4,5},{5,6},{6,7},{7,0},{8,9},{9,10},{10,1... | collective-permute-start | bytes 4616 | tf_op jit(solution)/shard_map/ppermute | solution.py:19
  8.2 11.6 %collective-permute-start.7 = (f32[8,8,6,1]{3,0,2,1:T(8,128)S(1)}, f32[8,8,6,1]{3,0,2,1:T(8,128)S(1)}, u32[]{:S(2)}, u32[]{:S(2)}) collective-permute-start(f32[8,8,6,1]{3,0,2,1:T(8,128)S(1)} %get-tuple-element.683), channel_id=1, source_target_pairs={{1,0},{2,1},{3,2},{4,3},{5,4},{6,5},{7,6},{0,7},{9,8},{10,9},{11,1... | collective-permute-start | bytes 4616 | tf_op jit(solution)/shard_map/ppermute | solution.py:20
  26.1 3.4 collective-permute-start
  26.3 3.2 collective-permute-start.1
  29.6 7.4 %collective-permute-start.2 = (f32[8,8,6,1]{3,0,2,1:T(8,128)S(1)}, f32[8,8,6,1]{3,0,2,1:T(8,128)S(1)}, u32[]{:S(2)}, u32[]{:S(2)}) collective-permute-start(f32[8,8,6,1]{3,0,2,1:T(8,128)S(1)} %get-tuple-element.788), channel_id=1, source_target_pairs={{1,0},{2,1},{3,2},{4,3},{5,4},{6,5},{7,6},{0,7},{9,8},{10,9},{11,1... | collective-permute-start | bytes 4616 | tf_op jit(solution)/shard_map/while/body/eval_jaxpr/ppermute | solution.py:20
  32.4 9.8 %collective-permute-start.3 = (f32[8,8,6,1]{3,0,2,1:T(8,128)S(1)}, f32[8,8,6,1]{3,0,2,1:T(8,128)S(1)}, u32[]{:S(2)}, u32[]{:S(2)}) collective-permute-start(f32[8,8,6,1]{3,0,2,1:T(8,128)S(1)} %get-tuple-element.789), channel_id=1, source_target_pairs={{0,1},{1,2},{2,3},{3,4},{4,5},{5,6},{6,7},{7,0},{8,9},{9,10},{10,1... | collective-permute-start | bytes 4616 | tf_op jit(solution)/shard_map/while/body/eval_jaxpr/ppermute | solution.py:19
  93.1 3.4 collective-permute-start
  93.2 3.5 collective-permute-start.1
  96.8 9.2 %collective-permute-start.2 = (f32[8,8,6,1]{3,0,2,1:T(8,128)S(1)}, f32[8,8,6,1]{3,0,2,1:T(8,128)S(1)}, u32[]{:S(2)}, u32[]{:S(2)}) collective-permute-start(f32[8,8,6,1]{3,0,2,1:T(8,128)S(1)} %get-tuple-element.788), channel_id=1, source_target_pairs={{1,0},{2,1},{3,2},{4,3},{5,4},{6,5},{7,6},{0,7},{9,8},{10,9},{11,1... | collective-permute-start | bytes 4616 | tf_op jit(solution)/shard_map/while/body/eval_jaxpr/ppermute | solution.py:20
  100.7 10.3 %collective-permute-start.3 = (f32[8,8,6,1]{3,0,2,1:T(8,128)S(1)}, f32[8,8,6,1]{3,0,2,1:T(8,128)S(1)}, u32[]{:S(2)}, u32[]{:S(2)}) collective-permute-start(f32[8,8,6,1]{3,0,2,1:T(8,128)S(1)} %get-tuple-element.789), channel_id=1, source_target_pairs={{0,1},{1,2},{2,3},{3,4},{4,5},{5,6},{6,7},{7,0},{8,9},{9,10},{10,1... | collective-permute-start | bytes 4616 | tf_op jit(solution)/shard_map/while/body/eval_jaxpr/ppermute | solution.py:19
  161.7 3.4 collective-permute-start
  161.8 3.5 collective-permute-start.1
  165.4 8.8 %collective-permute-start.2 = (f32[8,8,6,1]{3,0,2,1:T(8,128)S(1)}, f32[8,8,6,1]{3,0,2,1:T(8,128)S(1)}, u32[]{:S(2)}, u32[]{:S(2)}) collective-permute-start(f32[8,8,6,1]{3,0,2,1:T(8,128)S(1)} %get-tuple-element.788), channel_id=1, source_target_pairs={{1,0},{2,1},{3,2},{4,3},{5,4},{6,5},{7,6},{0,7},{9,8},{10,9},{11,1... | collective-permute-start | bytes 4616 | tf_op jit(solution)/shard_map/while/body/eval_jaxpr/ppermute | solution.py:20
  169.3 9.8 %collective-permute-start.3 = (f32[8,8,6,1]{3,0,2,1:T(8,128)S(1)}, f32[8,8,6,1]{3,0,2,1:T(8,128)S(1)}, u32[]{:S(2)}, u32[]{:S(2)}) collective-permute-start(f32[8,8,6,1]{3,0,2,1:T(8,128)S(1)} %get-tuple-element.789), channel_id=1, source_target_pairs={{0,1},{1,2},{2,3},{3,4},{4,5},{5,6},{6,7},{7,0},{8,9},{9,10},{10,1... | collective-permute-start | bytes 4616 | tf_op jit(solution)/shard_map/while/body/eval_jaxpr/ppermute | solution.py:19
  229.7 3.4 collective-permute-start
  229.7 3.5 collective-permute-start.1
  233.3 8.8 %collective-permute-start.2 = (f32[8,8,6,1]{3,0,2,1:T(8,128)S(1)}, f32[8,8,6,1]{3,0,2,1:T(8,128)S(1)}, u32[]{:S(2)}, u32[]{:S(2)}) collective-permute-start(f32[8,8,6,1]{3,0,2,1:T(8,128)S(1)} %get-tuple-element.788), channel_id=1, source_target_pairs={{1,0},{2,1},{3,2},{4,3},{5,4},{6,5},{7,6},{0,7},{9,8},{10,9},{11,1... | collective-permute-start | bytes 4616 | tf_op jit(solution)/shard_map/while/body/eval_jaxpr/ppermute | solution.py:20
  237.3 9.8 %collective-permute-start.3 = (f32[8,8,6,1]{3,0,2,1:T(8,128)S(1)}, f32[8,8,6,1]{3,0,2,1:T(8,128)S(1)}, u32[]{:S(2)}, u32[]{:S(2)}) collective-permute-start(f32[8,8,6,1]{3,0,2,1:T(8,128)S(1)} %get-tuple-element.789), channel_id=1, source_target_pairs={{0,1},{1,2},{2,3},{3,4},{4,5},{5,6},{6,7},{7,0},{8,9},{9,10},{10,1... | collective-permute-start | bytes 4616 | tf_op jit(solution)/shard_map/while/body/eval_jaxpr/ppermute | solution.py:19
  297.6 3.4 collective-permute-start
  297.7 3.5 collective-permute-start.1
  301.3 8.8 %collective-permute-start.2 = (f32[8,8,6,1]{3,0,2,1:T(8,128)S(1)}, f32[8,8,6,1]{3,0,2,1:T(8,128)S(1)}, u32[]{:S(2)}, u32[]{:S(2)}) collective-permute-start(f32[8,8,6,1]{3,0,2,1:T(8,128)S(1)} %get-tuple-element.788), channel_id=1, source_target_pairs={{1,0},{2,1},{3,2},{4,3},{5,4},{6,5},{7,6},{0,7},{9,8},{10,9},{11,1... | collective-permute-start | bytes 4616 | tf_op jit(solution)/shard_map/while/body/eval_jaxpr/ppermute | solution.py:20
  305.2 9.8 %collective-permute-start.3 = (f32[8,8,6,1]{3,0,2,1:T(8,128)S(1)}, f32[8,8,6,1]{3,0,2,1:T(8,128)S(1)}, u32[]{:S(2)}, u32[]{:S(2)}) collective-permute-start(f32[8,8,6,1]{3,0,2,1:T(8,128)S(1)} %get-tuple-element.789), channel_id=1, source_target_pairs={{0,1},{1,2},{2,3},{3,4},{4,5},{5,6},{6,7},{7,0},{8,9},{9,10},{10,1... | collective-permute-start | bytes 4616 | tf_op jit(solution)/shard_map/while/body/eval_jaxpr/ppermute | solution.py:19
  (26 other events, 53.2 us)
where the time goes:
time: 410 us; the launch traced here: 408 us
  blocking collectives  236 us (58%)
  waiting for transfers between devices  61.2 us (15%)
  matrix products  36.9 us (9%)
  starting transfers between devices  35.6 us (9%)
  local copies, waits for them, and re-layouts  15.6 us (4%)
  other arithmetic  13.3 us (3%)
  loops' own time  7.86 us (2%)
    psum x5, blocking collectives, advance(): lax.psum((local, local_total(pending * image), local_total(pending * pend...  196 us
    psum x1, blocking collectives, norm_scale(): squares = lax.psum(local_total(vector * vector), ('gx', 'gy'))  40.3 us
    ppermute x12, waiting for transfers between devices, extended(): before = lax.ppermute(last, axis, up)  34.7 us
    ppermute x12, starting transfers between devices, extended(): after = lax.ppermute(leading, axis, down)  32.4 us
    ppermute x12, waiting for transfers between devices, extended(): after = lax.ppermute(leading, axis, down)  26.5 us
    dot_general x5, matrix products, products(): per_cell = jnp.einsum('kqxy,qxy->kxy', basis, image, precision=highest)  13 us
    reduce_sum x12, other arithmetic, local_total(): return jnp.sum(jnp.sum(values, axis=0))  8.74 us
  transfers between devices with their start and end apart: 24, of which 23 were waited for; matrix products, arithmetic and copies ran while one was open for 1% of the time, Pallas kernels for 0%

commit v1 on v0

--- a/solution.py
+++ b/solution.py
@@ -71,7 +71,7 @@
 
 
 def norm_scale(vector, total):
-    squares = lax.psum(local_total(vector * vector), ("gx", "gy"))
+    squares = jnp.sum(lax.all_gather(local_total(vector * vector), ("gx", "gy")), axis=0)
     return jnp.sqrt(squares / total + FLOOR)
 
 

time: 410 us -> 410 us (level)
    psum x1 -> x0, blocking collectives: 40.3 us -> none  [norm_scale(): squares = lax.psum(local_total(vector * vector), ('gx', 'gy'))]
    unnamed x0 -> x1, blocking collectives: none -> 40.1 us
where the time goes in v1:
time: 410 us; the launch traced here: 409 us
  blocking collectives  236 us (58%)
  waiting for transfers between devices  61.1 us (15%)
  matrix products  36.9 us (9%)
  starting transfers between devices  35.7 us (9%)
  local copies, waits for them, and re-layouts  16.4 us (4%)
  other arithmetic  13.6 us (3%)
  loops' own time  7.87 us (2%)
    psum x5, blocking collectives, advance(): lax.psum((local, local_total(pending * image), local_total(pending * pend...  196 us
    unnamed x1, blocking collectives  40.1 us
    ppermute x12, waiting for transfers between devices, extended(): before = lax.ppermute(last, axis, up)  34.6 us
    ppermute x12, starting transfers between devices, extended(): after = lax.ppermute(leading, axis, down)  32.4 us
    ppermute x12, waiting for transfers between devices, extended(): after = lax.ppermute(leading, axis, down)  26.5 us
    dot_general x5, matrix products, products(): per_cell = jnp.einsum('kqxy,qxy->kxy', basis, image, precision=highest)  13 us
    reduce_sum x12, other arithmetic, local_total(): return jnp.sum(jnp.sum(values, axis=0))  8.45 us
  transfers between devices with their start and end apart: 24, of which 23 were waited for; matrix products, arithmetic and copies ran while one was open for 1% of the time, Pallas kernels for 0%

profile of v1, /device:TPU:0, one launch (start us, length us, event | category | flops | bytes accessed | tf_op | source)
XLA Modules:
  0.0 408.9 jit_solution(10659868201419584903)
XLA Ops:
  8.2 3.1 collective-permute-start.7
  12.3 4.8 %collective-permute-done.6 = f32[8,8,6,1]{3,0,2,1:T(8,128)S(1)} collective-permute-done((f32[8,8,6,1]{3,0,2,1:T(8,128)S(1)}, f32[8,8,6,1]{3,0,2,1:T(8,128)S(1)}, u32[]{:S(2)}, u32[]{:S(2)}) %collective-permute-start.6) | collective-permute-done | bytes 1568 | tf_op jit(solution)/shard_map/ppermute | solution.py:19
  25.9 339.2 %while.31 = (s32[]{:T(128)}, f32[6,64,4,128]{3,2,1,0:T(4,128)S(1)}, f32[6,5]{1,0:T(8,128)S(1)}, f32[64,4,128]{2,1,0:T(4,128)S(1)}, f32[64,4,128]{2,0,1:T(8,128)S...) while((s32[]{:T(128)}, f32[6,64,4,128]{3,2,1,0:T(4,128)S(1)}, ...), condition=%wide.region_6.7_spmd.clone.clone, body=%wide.region_0.6_spmd.clone.clone.sunk | while | flops 14006069 | bytes 9489035 | solution.py:121
  29.6 2.8 collective-permute-start.2
  32.7 4.3 %collective-permute-done.2 = f32[8,8,6,1]{3,0,2,1:T(8,128)S(1)} collective-permute-done((f32[8,8,6,1]{3,0,2,1:T(8,128)S(1)}, f32[8,8,6,1]{3,0,2,1:T(8,128)S(1)}, u32[]{:S(2)}, u32[]{:S(2)}) %collective-permute-start.2) | collective-permute-done | bytes 1568 | tf_op jit(solution)/shard_map/while/body/eval_jaxpr/ppermute | solution.py:20
  37.0 5.2 %collective-permute-done.3 = f32[8,8,6,1]{3,0,2,1:T(8,128)S(1)} collective-permute-done((f32[8,8,6,1]{3,0,2,1:T(8,128)S(1)}, f32[8,8,6,1]{3,0,2,1:T(8,128)S(1)}, u32[]{:S(2)}, u32[]{:S(2)}) %collective-permute-start.3) | collective-permute-done | bytes 1568 | tf_op jit(solution)/shard_map/while/body/eval_jaxpr/ppermute | solution.py:19
  49.8 39.3 %all-reduce.3 = (f32[]{:T(128)}, f32[6]{0:T(128)S(1)}, f32[]{:T(128)}) all-reduce(f32[]{:T(128)} %get-tuple-element.835, f32[6]{0:T(128)S(1)} %convolution_bitcast_fusion.2, f32[]{:T(128)} %fusion.189), channel_id=1, replica_groups=mesh['gx'=4,'gy'=8] {'gx','gy'}, use_global_device_ids=true, to_apply=%region_2.2 | all-reduce | flops 8 | bytes 64 | tf_op jit(solution)/shard_map/while/body/eval_jaxpr/psum | solution.py:108
  96.7 3.9 collective-permute-start.2
  100.9 4.9 %collective-permute-done.2 = f32[8,8,6,1]{3,0,2,1:T(8,128)S(1)} collective-permute-done((f32[8,8,6,1]{3,0,2,1:T(8,128)S(1)}, f32[8,8,6,1]{3,0,2,1:T(8,128)S(1)}, u32[]{:S(2)}, u32[]{:S(2)}) %collective-permute-start.2) | collective-permute-done | bytes 1568 | tf_op jit(solution)/shard_map/while/body/eval_jaxpr/ppermute | solution.py:20
  105.8 5.0 %collective-permute-done.3 = f32[8,8,6,1]{3,0,2,1:T(8,128)S(1)} collective-permute-done((f32[8,8,6,1]{3,0,2,1:T(8,128)S(1)}, f32[8,8,6,1]{3,0,2,1:T(8,128)S(1)}, u32[]{:S(2)}, u32[]{:S(2)}) %collective-permute-start.3) | collective-permute-done | bytes 1568 | tf_op jit(solution)/shard_map/while/body/eval_jaxpr/ppermute | solution.py:19
  118.5 39.2 %all-reduce.3 = (f32[]{:T(128)}, f32[6]{0:T(128)S(1)}, f32[]{:T(128)}) all-reduce(f32[]{:T(128)} %get-tuple-element.835, f32[6]{0:T(128)S(1)} %convolution_bitcast_fusion.2, f32[]{:T(128)} %fusion.189), channel_id=1, replica_groups=mesh['gx'=4,'gy'=8] {'gx','gy'}, use_global_device_ids=true, to_apply=%region_2.2 | all-reduce | flops 8 | bytes 64 | tf_op jit(solution)/shard_map/while/body/eval_jaxpr/psum | solution.py:108
  165.2 3.9 collective-permute-start.2
  169.4 4.6 %collective-permute-done.2 = f32[8,8,6,1]{3,0,2,1:T(8,128)S(1)} collective-permute-done((f32[8,8,6,1]{3,0,2,1:T(8,128)S(1)}, f32[8,8,6,1]{3,0,2,1:T(8,128)S(1)}, u32[]{:S(2)}, u32[]{:S(2)}) %collective-permute-start.2) | collective-permute-done | bytes 1568 | tf_op jit(solution)/shard_map/while/body/eval_jaxpr/ppermute | solution.py:20
  174.0 4.9 %collective-permute-done.3 = f32[8,8,6,1]{3,0,2,1:T(8,128)S(1)} collective-permute-done((f32[8,8,6,1]{3,0,2,1:T(8,128)S(1)}, f32[8,8,6,1]{3,0,2,1:T(8,128)S(1)}, u32[]{:S(2)}, u32[]{:S(2)}) %collective-permute-start.3) | collective-permute-done | bytes 1568 | tf_op jit(solution)/shard_map/while/body/eval_jaxpr/ppermute | solution.py:19
  186.5 39.0 %all-reduce.3 = (f32[]{:T(128)}, f32[6]{0:T(128)S(1)}, f32[]{:T(128)}) all-reduce(f32[]{:T(128)} %get-tuple-element.835, f32[6]{0:T(128)S(1)} %convolution_bitcast_fusion.2, f32[]{:T(128)} %fusion.189), channel_id=1, replica_groups=mesh['gx'=4,'gy'=8] {'gx','gy'}, use_global_device_ids=true, to_apply=%region_2.2 | all-reduce | flops 8 | bytes 64 | tf_op jit(solution)/shard_map/while/body/eval_jaxpr/psum | solution.py:108
  233.1 3.9 collective-permute-start.2
  237.3 4.6 %collective-permute-done.2 = f32[8,8,6,1]{3,0,2,1:T(8,128)S(1)} collective-permute-done((f32[8,8,6,1]{3,0,2,1:T(8,128)S(1)}, f32[8,8,6,1]{3,0,2,1:T(8,128)S(1)}, u32[]{:S(2)}, u32[]{:S(2)}) %collective-permute-start.2) | collective-permute-done | bytes 1568 | tf_op jit(solution)/shard_map/while/body/eval_jaxpr/ppermute | solution.py:20
  241.9 4.9 %collective-permute-done.3 = f32[8,8,6,1]{3,0,2,1:T(8,128)S(1)} collective-permute-done((f32[8,8,6,1]{3,0,2,1:T(8,128)S(1)}, f32[8,8,6,1]{3,0,2,1:T(8,128)S(1)}, u32[]{:S(2)}, u32[]{:S(2)}) %collective-permute-start.3) | collective-permute-done | bytes 1568 | tf_op jit(solution)/shard_map/while/body/eval_jaxpr/ppermute | solution.py:19
  254.4 39.0 %all-reduce.3 = (f32[]{:T(128)}, f32[6]{0:T(128)S(1)}, f32[]{:T(128)}) all-reduce(f32[]{:T(128)} %get-tuple-element.835, f32[6]{0:T(128)S(1)} %convolution_bitcast_fusion.2, f32[]{:T(128)} %fusion.189), channel_id=1, replica_groups=mesh['gx'=4,'gy'=8] {'gx','gy'}, use_global_device_ids=true, to_apply=%region_2.2 | all-reduce | flops 8 | bytes 64 | tf_op jit(solution)/shard_map/while/body/eval_jaxpr/psum | solution.py:108
  301.0 3.9 collective-permute-start.2
  305.2 4.6 %collective-permute-done.2 = f32[8,8,6,1]{3,0,2,1:T(8,128)S(1)} collective-permute-done((f32[8,8,6,1]{3,0,2,1:T(8,128)S(1)}, f32[8,8,6,1]{3,0,2,1:T(8,128)S(1)}, u32[]{:S(2)}, u32[]{:S(2)}) %collective-permute-start.2) | collective-permute-done | bytes 1568 | tf_op jit(solution)/shard_map/while/body/eval_jaxpr/ppermute | solution.py:20
  309.8 4.9 %collective-permute-done.3 = f32[8,8,6,1]{3,0,2,1:T(8,128)S(1)} collective-permute-done((f32[8,8,6,1]{3,0,2,1:T(8,128)S(1)}, f32[8,8,6,1]{3,0,2,1:T(8,128)S(1)}, u32[]{:S(2)}, u32[]{:S(2)}) %collective-permute-start.3) | collective-permute-done | bytes 1568 | tf_op jit(solution)/shard_map/while/body/eval_jaxpr/ppermute | solution.py:19
  322.3 39.0 %all-reduce.3 = (f32[]{:T(128)}, f32[6]{0:T(128)S(1)}, f32[]{:T(128)}) all-reduce(f32[]{:T(128)} %get-tuple-element.835, f32[6]{0:T(128)S(1)} %convolution_bitcast_fusion.2, f32[]{:T(128)} %fusion.189), channel_id=1, replica_groups=mesh['gx'=4,'gy'=8] {'gx','gy'}, use_global_device_ids=true, to_apply=%region_2.2 | all-reduce | flops 8 | bytes 64 | tf_op jit(solution)/shard_map/while/body/eval_jaxpr/psum | solution.py:108
  366.6 40.1 %all-reduce = f32[32]{0:T(128)S(1)} all-reduce(f32[32]{0:T(128)S(1)} %dynamic-update-slice.59), channel_id=1, replica_groups=mesh['gx'=4,'gy'=8] {'gx','gy'}, use_global_device_ids=true, to_apply=%add | all-reduce | flops 32 | bytes 256
  (333 shorter events, 89.3 us)
Async XLA Ops:
  1.6 4.1 collective-permute-start.4
  2.2 3.7 collective-permute-start.5
  6.0 11.1 %collective-permute-start.6 = (f32[8,8,6,1]{3,0,2,1:T(8,128)S(1)}, f32[8,8,6,1]{3,0,2,1:T(8,128)S(1)}, u32[]{:S(2)}, u32[]{:S(2)}) collective-permute-start(f32[8,8,6,1]{3,0,2,1:T(8,128)S(1)} %get-tuple-element.682), channel_id=1, source_target_pairs={{0,1},{1,2},{2,3},{3,4},{4,5},{5,6},{6,7},{7,0},{8,9},{9,10},{10,1... | collective-permute-start | bytes 4616 | tf_op jit(solution)/shard_map/ppermute | solution.py:19
  8.2 11.6 %collective-permute-start.7 = (f32[8,8,6,1]{3,0,2,1:T(8,128)S(1)}, f32[8,8,6,1]{3,0,2,1:T(8,128)S(1)}, u32[]{:S(2)}, u32[]{:S(2)}) collective-permute-start(f32[8,8,6,1]{3,0,2,1:T(8,128)S(1)} %get-tuple-element.683), channel_id=1, source_target_pairs={{1,0},{2,1},{3,2},{4,3},{5,4},{6,5},{7,6},{0,7},{9,8},{10,9},{11,1... | collective-permute-start | bytes 4616 | tf_op jit(solution)/shard_map/ppermute | solution.py:20
  26.0 3.4 collective-permute-start
  26.3 3.2 collective-permute-start.1
  29.6 7.4 %collective-permute-start.2 = (f32[8,8,6,1]{3,0,2,1:T(8,128)S(1)}, f32[8,8,6,1]{3,0,2,1:T(8,128)S(1)}, u32[]{:S(2)}, u32[]{:S(2)}) collective-permute-start(f32[8,8,6,1]{3,0,2,1:T(8,128)S(1)} %get-tuple-element.788), channel_id=1, source_target_pairs={{1,0},{2,1},{3,2},{4,3},{5,4},{6,5},{7,6},{0,7},{9,8},{10,9},{11,1... | collective-permute-start | bytes 4616 | tf_op jit(solution)/shard_map/while/body/eval_jaxpr/ppermute | solution.py:20
  32.4 9.8 %collective-permute-start.3 = (f32[8,8,6,1]{3,0,2,1:T(8,128)S(1)}, f32[8,8,6,1]{3,0,2,1:T(8,128)S(1)}, u32[]{:S(2)}, u32[]{:S(2)}) collective-permute-start(f32[8,8,6,1]{3,0,2,1:T(8,128)S(1)} %get-tuple-element.789), channel_id=1, source_target_pairs={{0,1},{1,2},{2,3},{3,4},{4,5},{5,6},{6,7},{7,0},{8,9},{9,10},{10,1... | collective-permute-start | bytes 4616 | tf_op jit(solution)/shard_map/while/body/eval_jaxpr/ppermute | solution.py:19
  93.0 3.4 collective-permute-start
  93.1 3.5 collective-permute-start.1
  96.7 9.2 %collective-permute-start.2 = (f32[8,8,6,1]{3,0,2,1:T(8,128)S(1)}, f32[8,8,6,1]{3,0,2,1:T(8,128)S(1)}, u32[]{:S(2)}, u32[]{:S(2)}) collective-permute-start(f32[8,8,6,1]{3,0,2,1:T(8,128)S(1)} %get-tuple-element.788), channel_id=1, source_target_pairs={{1,0},{2,1},{3,2},{4,3},{5,4},{6,5},{7,6},{0,7},{9,8},{10,9},{11,1... | collective-permute-start | bytes 4616 | tf_op jit(solution)/shard_map/while/body/eval_jaxpr/ppermute | solution.py:20
  100.6 10.3 %collective-permute-start.3 = (f32[8,8,6,1]{3,0,2,1:T(8,128)S(1)}, f32[8,8,6,1]{3,0,2,1:T(8,128)S(1)}, u32[]{:S(2)}, u32[]{:S(2)}) collective-permute-start(f32[8,8,6,1]{3,0,2,1:T(8,128)S(1)} %get-tuple-element.789), channel_id=1, source_target_pairs={{0,1},{1,2},{2,3},{3,4},{4,5},{5,6},{6,7},{7,0},{8,9},{9,10},{10,1... | collective-permute-start | bytes 4616 | tf_op jit(solution)/shard_map/while/body/eval_jaxpr/ppermute | solution.py:19
  161.5 3.4 collective-permute-start
  161.6 3.5 collective-permute-start.1
  165.2 8.8 %collective-permute-start.2 = (f32[8,8,6,1]{3,0,2,1:T(8,128)S(1)}, f32[8,8,6,1]{3,0,2,1:T(8,128)S(1)}, u32[]{:S(2)}, u32[]{:S(2)}) collective-permute-start(f32[8,8,6,1]{3,0,2,1:T(8,128)S(1)} %get-tuple-element.788), channel_id=1, source_target_pairs={{1,0},{2,1},{3,2},{4,3},{5,4},{6,5},{7,6},{0,7},{9,8},{10,9},{11,1... | collective-permute-start | bytes 4616 | tf_op jit(solution)/shard_map/while/body/eval_jaxpr/ppermute | solution.py:20
  169.1 9.8 %collective-permute-start.3 = (f32[8,8,6,1]{3,0,2,1:T(8,128)S(1)}, f32[8,8,6,1]{3,0,2,1:T(8,128)S(1)}, u32[]{:S(2)}, u32[]{:S(2)}) collective-permute-start(f32[8,8,6,1]{3,0,2,1:T(8,128)S(1)} %get-tuple-element.789), channel_id=1, source_target_pairs={{0,1},{1,2},{2,3},{3,4},{4,5},{5,6},{6,7},{7,0},{8,9},{9,10},{10,1... | collective-permute-start | bytes 4616 | tf_op jit(solution)/shard_map/while/body/eval_jaxpr/ppermute | solution.py:19
  229.4 3.4 collective-permute-start
  229.5 3.5 collective-permute-start.1
  233.1 8.8 %collective-permute-start.2 = (f32[8,8,6,1]{3,0,2,1:T(8,128)S(1)}, f32[8,8,6,1]{3,0,2,1:T(8,128)S(1)}, u32[]{:S(2)}, u32[]{:S(2)}) collective-permute-start(f32[8,8,6,1]{3,0,2,1:T(8,128)S(1)} %get-tuple-element.788), channel_id=1, source_target_pairs={{1,0},{2,1},{3,2},{4,3},{5,4},{6,5},{7,6},{0,7},{9,8},{10,9},{11,1... | collective-permute-start | bytes 4616 | tf_op jit(solution)/shard_map/while/body/eval_jaxpr/ppermute | solution.py:20
  237.0 9.8 %collective-permute-start.3 = (f32[8,8,6,1]{3,0,2,1:T(8,128)S(1)}, f32[8,8,6,1]{3,0,2,1:T(8,128)S(1)}, u32[]{:S(2)}, u32[]{:S(2)}) collective-permute-start(f32[8,8,6,1]{3,0,2,1:T(8,128)S(1)} %get-tuple-element.789), channel_id=1, source_target_pairs={{0,1},{1,2},{2,3},{3,4},{4,5},{5,6},{6,7},{7,0},{8,9},{9,10},{10,1... | collective-permute-start | bytes 4616 | tf_op jit(solution)/shard_map/while/body/eval_jaxpr/ppermute | solution.py:19
  297.3 3.4 collective-permute-start
  297.4 3.5 collective-permute-start.1
  301.0 8.8 %collective-permute-start.2 = (f32[8,8,6,1]{3,0,2,1:T(8,128)S(1)}, f32[8,8,6,1]{3,0,2,1:T(8,128)S(1)}, u32[]{:S(2)}, u32[]{:S(2)}) collective-permute-start(f32[8,8,6,1]{3,0,2,1:T(8,128)S(1)} %get-tuple-element.788), channel_id=1, source_target_pairs={{1,0},{2,1},{3,2},{4,3},{5,4},{6,5},{7,6},{0,7},{9,8},{10,9},{11,1... | collective-permute-start | bytes 4616 | tf_op jit(solution)/shard_map/while/body/eval_jaxpr/ppermute | solution.py:20
  304.9 9.8 %collective-permute-start.3 = (f32[8,8,6,1]{3,0,2,1:T(8,128)S(1)}, f32[8,8,6,1]{3,0,2,1:T(8,128)S(1)}, u32[]{:S(2)}, u32[]{:S(2)}) collective-permute-start(f32[8,8,6,1]{3,0,2,1:T(8,128)S(1)} %get-tuple-element.789), channel_id=1, source_target_pairs={{0,1},{1,2},{2,3},{3,4},{4,5},{5,6},{6,7},{7,0},{8,9},{9,10},{10,1... | collective-permute-start | bytes 4616 | tf_op jit(solution)/shard_map/while/body/eval_jaxpr/ppermute | solution.py:19
  (26 other events, 54.7 us)
